TPU v7x, 32 devices: a whole 2x2x4 slice. The times are simulated.
32 devices in a mesh: dp: 2 (over x), pp: 4 (over z), ep: 4 (over y, core).
Axes of the slice: x: 2, y: 2, z: 4, core: 2. Of those that a mesh axis runs over, the one named last changes fastest.
Arguments:
- x_a: bfloat16 [8, 4, 128, 768], P(('dp', 'pp'), 'ep'), parts along dimension 0
- x_b: bfloat16 [8, 4, 128, 768], P(('dp', 'pp'), 'ep'), parts along dimension 0
- g_b: bfloat16 [8, 4, 128, 768], P(('dp', 'pp'), 'ep'), parts along dimension 0
- ids_a: int32 [8, 4, 128, 2], P(('dp', 'pp'), 'ep'), parts along dimension 0
- ids_b: int32 [8, 4, 128, 2], P(('dp', 'pp'), 'ep'), parts along dimension 0
- count_a: int32 [8, 4, 8], P(('dp', 'pp'), 'ep'), parts along dimension 0
- count_b: int32 [8, 4, 8], P(('dp', 'pp'), 'ep'), parts along dimension 0
- gain_1: bfloat16 [4, 768], P('pp')
- gain_2: bfloat16 [4, 768], P('pp')
- w_q: bfloat16 [4, 768, 6, 128], P('pp')
- w_k: bfloat16 [4, 768, 1, 128], P('pp')
- w_v: bfloat16 [4, 768, 1, 128], P('pp')
- w_o: bfloat16 [4, 6, 128, 768], P('pp')
- w_r: bfloat16 [4, 768, 8], P('pp')
- w_1: bfloat16 [4, 8, 768, 2048], P('pp', 'ep')
- w_3: bfloat16 [4, 8, 768, 2048], P('pp', 'ep')
- w_2: bfloat16 [4, 8, 2048, 768], P('pp', 'ep')
Outputs:
- output 1: bfloat16 [8, 4, 128, 768], P(('dp', 'pp'), 'ep'), parts along dimension 0
- output 2: bfloat16 [8, 4, 128, 768], P(('dp', 'pp'), 'ep'), parts along dimension 0
- output 3: float32 [8, 768], P(('dp', 'pp')), parts along dimension 0
- output 4: float32 [8, 768], P(('dp', 'pp')), parts along dimension 0
- output 5: float32 [8, 768, 6, 128], P(('dp', 'pp')), parts along dimension 0
- output 6: float32 [8, 768, 1, 128], P(('dp', 'pp')), parts along dimension 0
- output 7: float32 [8, 768, 1, 128], P(('dp', 'pp')), parts along dimension 0
- output 8: float32 [8, 6, 128, 768], P(('dp', 'pp')), parts along dimension 0
- output 9: float32 [8, 768, 8], P(('dp', 'pp')), parts along dimension 0
- output 10: float32 [8, 8, 768, 2048], P(('dp', 'pp'), 'ep'), parts along dimension 0
- output 11: float32 [8, 8, 768, 2048], P(('dp', 'pp'), 'ep'), parts along dimension 0
- output 12: float32 [8, 8, 2048, 768], P(('dp', 'pp'), 'ep'), parts along dimension 0
There are 2 independent parts. A program takes and returns all parts, laid end to end along the dimension named above; an argument that names none is the same for every part.
All inputs are finite; a program needn't handle non-finite values.
Results may differ from a plain program's by a relative error of at most 0.019921.
Values are sent between devices in bfloat16 or wider.
A program may use at most 1 GiB of HBM per device.

v0:
```python
import functools

import jax
import jax.numpy as jnp
from jax import lax
from jax.experimental import pallas as pl
from jax.experimental.pallas import tpu as pltpu
from jax.sharding import PartitionSpec as P

NORM_EPS = 1e-6
MASK_VALUE = -1e30
F32 = jnp.float32
BF16 = jnp.bfloat16
MESH = pl.DeviceIdType.MESH
VMEM = pltpu.VMEM
FFN_TILE = 256
LANES = 128
ROW_SIZES = (128, 192, 320, 512)
RING = 3
CHUNKS = 4
HEAD_VMEM = 34 * 2 ** 20
MOE_VMEM = 44 * 2 ** 20
TAIL_VMEM = 30 * 2 ** 20
DENSE_VMEM = 24 * 2 ** 20


def dot_nn(lhs, rhs):
    return lax.dot_general(lhs, rhs, (((1,), (0,)), ((), ())), preferred_element_type=F32)


def dot_nt(lhs, rhs):
    return lax.dot_general(lhs, rhs, (((1,), (1,)), ((), ())), preferred_element_type=F32)


def dot_tn(lhs, rhs):
    return lax.dot_general(lhs, rhs, (((0,), (0,)), ((), ())), preferred_element_type=F32)


def ep_peers():
    me = lax.axis_index('ep')
    partner = me + 1 - 2 * lax.rem(me, 2)
    across = lax.rem(me + 2, 4)
    diag = lax.rem(partner + 2, 4)
    return me, partner, across, diag


def greet(peers):
    barrier = pltpu.get_barrier_semaphore()
    for peer in peers:
        pl.semaphore_signal(barrier, inc=1, device_id=peer, device_id_type=MESH)
    pl.semaphore_wait(barrier, len(peers))


def push(src, dst, sems, idx, peer):
    return pltpu.make_async_remote_copy(src_ref=src, dst_ref=dst, send_sem=sems[0].at[idx], recv_sem=sems[1].at[idx],
                                        device_id=peer, device_id_type=MESH)


def stack_heads(wide, heads, head_dim):
    return jnp.concatenate([wide[:, h * head_dim:(h + 1) * head_dim] for h in range(heads)], axis=0)


def unstack_heads(tall, heads, seq_len):
    return jnp.concatenate([tall[h * seq_len:(h + 1) * seq_len] for h in range(heads)], axis=1)


def rms_inv(x_f32):
    return lax.rsqrt(jnp.mean(x_f32 * x_f32, axis=-1, keepdims=True) + NORM_EPS)


def attention_rows(x_bf, gain, wq, wk, wv, wo, n_seq, heads):
    seq_len, head_dim = x_bf.shape[0] // n_seq, wk.shape[1]
    x_f32 = x_bf.astype(F32)
    normed = (x_f32 * rms_inv(x_f32) * gain).astype(BF16)
    query = dot_nn(normed, wq).astype(BF16)
    key = dot_nn(normed, wk).astype(BF16)
    value = dot_nn(normed, wv).astype(BF16)
    row = lax.rem(lax.broadcasted_iota(jnp.int32, (heads * seq_len, seq_len), 0), seq_len)
    col = lax.broadcasted_iota(jnp.int32, (heads * seq_len, seq_len), 1)
    causal = row >= col
    outs, probs_all = [], []
    for s in range(n_seq):
        rows = slice(s * seq_len, (s + 1) * seq_len)
        scores = dot_nt(stack_heads(query[rows], heads, head_dim), key[rows]) * head_dim ** -0.5
        scores = jnp.where(causal, scores, MASK_VALUE)
        expd = jnp.exp(scores - jnp.max(scores, axis=-1, keepdims=True))
        probs = expd / jnp.sum(expd, axis=-1, keepdims=True)
        probs_all.append(probs)
        outs.append(unstack_heads(dot_nn(probs.astype(BF16), value[rows]).astype(BF16), heads, seq_len))
    attn = jnp.concatenate(outs, axis=0)
    hidden = (x_f32 + dot_nn(attn, wo)).astype(BF16)
    return hidden, (normed, query, key, value, probs_all, attn)


def route_rows(hidden, gain, wr, cols, counts, base, n_seq):
    seq_len = hidden.shape[0] // n_seq
    h_f32 = hidden.astype(F32)
    normed = (h_f32 * rms_inv(h_f32) * gain).astype(BF16)
    logits = dot_nn(normed, wr)
    lane = lax.broadcasted_iota(jnp.int32, (seq_len, LANES), 1).astype(F32)
    lower = (lax.broadcasted_iota(jnp.int32, (seq_len, seq_len), 0)
             > lax.broadcasted_iota(jnp.int32, (seq_len, seq_len), 1)).astype(F32).astype(BF16)
    weights, masks, routes = [], [], []
    for s in range(n_seq):
        id0, id1 = cols[s][base], cols[s][base + 1]
        hot0, hot1 = (lane == id0).astype(F32), (lane == id1).astype(F32)
        rank = dot_nn(lower, (hot0 + hot1).astype(BF16))
        rank1 = rank + (id0 == id1).astype(F32)
        kept0 = hot0 * (rank < counts[s]).astype(F32)
        kept1 = hot1 * (rank1 < counts[s]).astype(F32)
        part = logits[s * seq_len:(s + 1) * seq_len]
        sel0 = jnp.sum(jnp.where(hot0 > 0, part, 0.0), axis=-1, keepdims=True)
        sel1 = jnp.sum(jnp.where(hot1 > 0, part, 0.0), axis=-1, keepdims=True)
        top = jnp.maximum(sel0, sel1)
        exp0, exp1 = jnp.exp(sel0 - top), jnp.exp(sel1 - top)
        gate0, gate1 = exp0 / (exp0 + exp1), exp1 / (exp0 + exp1)
        weights.append(kept0 * gate0 + kept1 * gate1)
        masks.append(jnp.maximum(kept0, kept1))
        keep0 = jnp.sum(kept0, axis=-1, keepdims=True)
        keep1 = jnp.sum(kept1, axis=-1, keepdims=True)
        route = jnp.zeros((seq_len, LANES), F32)
        for i, item in enumerate((id0, id1, gate0, gate1, keep0, keep1)):
            route = jnp.where(lane == i, item, route)
        routes.append(route)
    return normed, jnp.concatenate(weights, 0), jnp.concatenate(masks, 0), jnp.concatenate(routes, 0)


def head_kernel(n_ep, heads, ida_hbm, idb_hbm, cta_hbm, ctb_hbm, xa_hbm, xb_hbm, gb_hbm, gain1_hbm, gain2_hbm, wq_hbm, wk_hbm,
                wv_hbm, wo_hbm, wr_hbm,
                xb_all, gb_all, n2a_ref, n2b_ref, wta_ref, ma_ref, wtb_ref, mb_ref, rtb_ref, ha_ref, hb_ref,
                n1_ref, q_ref, k_ref, v_ref, p_ref, o_ref,
                xa_all, pk_ref, pk_all, ida_ref, idb_ref, cta_ref, ctb_ref, gain1_ref, gain2_ref, wq_s, wk_ref, wv_ref, wo_ref,
                wr_ref, wr_s, load_sem, send_sem, recv_sem):
    me, partner, across, diag = ep_peers()
    sems = (send_sem, recv_sem)
    seq_len = xb_all.shape[1]
    moves = [(ida_hbm, ida_ref), (idb_hbm, idb_ref), (cta_hbm, cta_ref), (ctb_hbm, ctb_ref), (xb_hbm, xb_all.at[me]),
             (xa_hbm, xa_all.at[me]), (gb_hbm, gb_all.at[me]), (gain1_hbm, gain1_ref), (gain2_hbm, gain2_ref)]
    moves += [(wq_hbm.at[h], wq_s.at[:, pl.ds(h * LANES, LANES)]) for h in range(heads)]
    moves += [(wk_hbm, wk_ref), (wv_hbm, wv_ref), (wo_hbm, wo_ref), (wr_hbm, wr_ref)]
    loads = [pltpu.make_async_copy(src, dst, load_sem.at[i]) for i, (src, dst) in enumerate(moves)]
    for load in loads:
        load.start()
    greet(({'ep': partner}, {'ep': across}))
    landing = (pk_all, xb_all, xa_all, gb_all)
    far, near, relay = [], [], []
    for i in range(4):
        own = pk_ref if i == 0 else landing[i].at[me]
        far.append(push(own, landing[i].at[me], sems, 3 * i, {'ep': across}))
        near.append(push(own, landing[i].at[me], sems, 3 * i + 1, {'ep': partner}))
        relay.append(push(landing[i].at[across], landing[i].at[across], sems, 3 * i + 2, {'ep': partner}))

    def leave(i):
        far[i].start()
        near[i].start()

    for load in loads[0:4]:
        load.wait()
    pk_ref[...] = jnp.zeros_like(pk_ref)
    pk_ref[0:2, :] = ida_ref[...]
    pk_ref[2:4, :] = idb_ref[...]
    pk_ref[4:5, 0:cta_ref.shape[1]] = cta_ref[...]
    pk_ref[5:6, 0:ctb_ref.shape[1]] = ctb_ref[...]
    pk_all[me] = pk_ref[...]
    loads[4].wait()
    leave(1)
    leave(0)
    loads[5].wait()
    leave(2)
    loads[6].wait()
    leave(3)
    for load in loads[7:]:
        load.wait()
    wr_s[...] = jnp.zeros_like(wr_s)
    wr_s[0:wr_ref.shape[0], :] = wr_ref[...]
    wr = wr_s[...].T
    gain1, gain2 = gain1_ref[...].astype(F32), gain2_ref[...].astype(F32)

    def pair_b(pair):
        x_pair = jnp.concatenate([xb_all[s] for s in pair], axis=0)
        hidden, (normed, query, key, value, probs, attn) = attention_rows(
            x_pair, gain1, wq_s[...], wk_ref[...], wv_ref[...], wo_ref[...], len(pair), heads)
        cols, counts = routing_of(pair)
        routed = route_rows(hidden, gain2, wr, cols, [c[1] for c in counts], 2, len(pair))
        for n, s in enumerate(pair):
            rows, part = pl.ds(pl.multiple_of(s * seq_len, seq_len), seq_len), slice(n * seq_len, (n + 1) * seq_len)
            n1_ref[rows, :], q_ref[rows, :], k_ref[rows, :] = normed[part], query[part], key[part]
            v_ref[rows, :], o_ref[rows, :], hb_ref[rows, :] = value[part], attn[part], hidden[part]
            p_ref[s] = probs[n]
            n2b_ref[rows, :], wtb_ref[rows, :], mb_ref[rows, :], rtb_ref[rows, :] = [item[part] for item in routed]

    def pair_a(pair):
        x_pair = jnp.concatenate([xa_all[s] for s in pair], axis=0)
        hidden, _ = attention_rows(x_pair, gain1, wq_s[...], wk_ref[...], wv_ref[...], wo_ref[...], len(pair), heads)
        cols, counts = routing_of(pair)
        routed = route_rows(hidden, gain2, wr, cols, [c[0] for c in counts], 0, len(pair))
        for n, s in enumerate(pair):
            rows, part = pl.ds(pl.multiple_of(s * seq_len, seq_len), seq_len), slice(n * seq_len, (n + 1) * seq_len)
            ha_ref[rows, :] = hidden[part]
            n2a_ref[rows, :], wta_ref[rows, :], ma_ref[rows, :] = [item[part] for item in routed[:3]]

    def routing_of(pair):
        packed = [pk_all[s].astype(F32) for s in pair]
        flat = jnp.concatenate(packed + [jnp.zeros((LANES - 8 * len(pair), LANES), F32)], axis=0).T
        cols = [[flat[:, 8 * n + r:8 * n + r + 1] for r in range(4)] for n in range(len(pair))]
        return cols, [(item[4:5, :], item[5:6, :]) for item in packed]

    near[0].wait_recv()
    near[1].wait_recv()
    pair_b((me, partner))
    far[0].wait_recv()
    relay[0].start()
    far[1].wait_recv()
    relay[1].start()
    near[2].wait_recv()
    pair_a((me, partner))
    relay[0].wait_recv()
    relay[1].wait_recv()
    far[2].wait_recv()
    relay[2].start()
    pair_b((across, diag))
    relay[2].wait_recv()
    far[3].wait_recv()
    relay[3].start()
    pair_a((across, diag))
    near[3].wait_recv()
    relay[3].wait_recv()
    for i in range(4):
        far[i].wait_send()
        near[i].wait_send()
        relay[i].wait_send()


def moe_kernel(e_local, n2a_ref, n2b_ref, g_ref, wta_ref, ma_ref, wtb_ref, mb_ref, w1_hbm, w3_hbm, w2_hbm,
               ra_ref, rb_ref, rd_ref, dw1_ref, dw3_ref, dw2_ref, x_a, x_b, xbt, dexp, acc_a, acc_b, dacc, put_a, put_b, wcol, dots, ring_1, ring_3, ring_2,
               w1_all, w3_all, w2_all, ring_sem, load_sem, blocks):
    expert, tile = pl.program_id(0), pl.program_id(1)
    n_tile = pl.num_programs(1)
    step = expert * n_tile + tile
    slot = lax.rem(step, RING)

    def leaving(step, slot):
        expert, start = step // n_tile, pl.multiple_of(lax.rem(step, n_tile) * FFN_TILE, FFN_TILE)
        span = pl.ds(start, FFN_TILE)
        return [pltpu.make_async_copy(ring_1.at[slot], dw1_ref.at[expert, :, span], ring_sem.at[slot, 0]),
                pltpu.make_async_copy(ring_3.at[slot], dw3_ref.at[expert, :, span], ring_sem.at[slot, 1]),
                pltpu.make_async_copy(ring_2.at[slot], dw2_ref.at[expert, span, :], ring_sem.at[slot, 2])]

    def coming(step, slot):
        expert, start = step // n_tile, pl.multiple_of(lax.rem(step, n_tile) * FFN_TILE, FFN_TILE)
        span = pl.ds(start, FFN_TILE)
        return [pltpu.make_async_copy(w1_hbm.at[expert, :, span], w1_all.at[slot], load_sem.at[slot, 0]),
                pltpu.make_async_copy(w3_hbm.at[expert, :, span], w3_all.at[slot], load_sem.at[slot, 1]),
                pltpu.make_async_copy(w2_hbm.at[expert, span, :], w2_all.at[slot], load_sem.at[slot, 2])]

    @pl.when(step == 0)
    def _():
        for ahead in range(RING):
            for copy in coming(ahead, ahead):
                copy.start()

    n_tok, d_model = n2a_ref.shape
    here = lax.axis_index('ep') * e_local + expert

    def by_rows(which, work):
        for rows in ROW_SIZES:
            pl.when(blocks[which] == rows)(functools.partial(work, rows))

    @pl.when(tile == 0)
    def _():
        mine = lax.broadcasted_iota(jnp.int32, (n_tok, LANES), 1) == here
        mine_t = lax.broadcasted_iota(jnp.int32, (LANES, n_tok), 0) == here
        lower = (lax.broadcasted_iota(jnp.int32, (n_tok, n_tok), 0)
                 > lax.broadcasted_iota(jnp.int32, (n_tok, n_tok), 1)).astype(F32).astype(BF16)
        slot_col = lax.broadcasted_iota(jnp.int32, (n_tok, n_tok), 1).astype(F32)
        slot_row = lax.broadcasted_iota(jnp.int32, (n_tok, n_tok), 0).astype(F32)

        def plan(which, mask_ref, put):
            mask = mask_ref[...]
            place = jnp.where(mask > 0, dot_nn(lower, mask.astype(BF16)), -1.0)
            place_col = jnp.sum(jnp.where(mine, place, 0.0), axis=-1, keepdims=True)
            place_row = jnp.sum(jnp.where(mine_t, place.T, 0.0), axis=0, keepdims=True)
            put[...] = (slot_col == place_col).astype(F32).astype(BF16)
            total = jnp.sum(jnp.where(mine, mask, 0.0)).astype(jnp.int32)
            size = jnp.int32(n_tok)
            for rows in ROW_SIZES[-2::-1]:
                size = jnp.where(total <= rows, rows, size)
            blocks[which] = size
            return (slot_row == place_row).astype(F32).astype(BF16)

        take_a, take_b = plan(0, ma_ref, put_a), plan(1, mb_ref, put_b)
        wcol[...] = jnp.broadcast_to(jnp.sum(jnp.where(mine, wta_ref[...], 0.0), axis=-1, keepdims=True), (n_tok, LANES))
        wt_b = jnp.sum(jnp.where(mine, wtb_ref[...], 0.0), axis=-1, keepdims=True)
        scaled = (wt_b * g_ref[...].astype(F32)).astype(BF16)

        def fetch_a(rows):
            x_a[0:rows, :] = dot_nn(take_a[0:rows], n2a_ref[...]).astype(BF16)
            acc_a[0:rows, :] = jnp.zeros((rows, d_model), F32)

        def fetch_b(rows):
            fetched = dot_nn(take_b[0:rows], n2b_ref[...])
            x_b[0:rows, :] = fetched.astype(BF16)
            xbt[:, 0:rows] = fetched.T.astype(BF16)
            dexp[0:rows, :] = dot_nn(take_b[0:rows], scaled).astype(BF16)
            acc_b[0:rows, :] = jnp.zeros((rows, d_model), F32)
            dacc[0:rows, :] = jnp.zeros((rows, d_model), F32)

        by_rows(0, fetch_a)
        by_rows(1, fetch_b)

    @pl.when((tile == 0) & (expert == 0))
    def _():
        ra_ref[...] = jnp.zeros_like(ra_ref)
        rb_ref[...] = jnp.zeros_like(rb_ref)
        dots[...] = jnp.zeros_like(dots)

    for copy in coming(step, slot):
        copy.wait()

    @pl.when(step >= RING)
    def _():
        for copy in leaving(step - RING, slot):
            copy.wait()

    w1_ref, w3_ref, w2_ref = w1_all.at[slot], w3_all.at[slot], w2_all.at[slot]

    def forward(x, rows):
        gate_pre, up_pre = dot_nn(x[0:rows, :], w1_ref[...]), dot_nn(x[0:rows, :], w3_ref[...])
        sig = jax.nn.sigmoid(gate_pre)
        return gate_pre, up_pre, sig, (gate_pre * sig * up_pre).astype(BF16)

    def run_a(rows):
        act = forward(x_a, rows)[3]
        acc_a[0:rows, :] += dot_nn(act, w2_ref[...])

    def run_b(rows):
        gate_pre, up_pre, sig, act = forward(x_b, rows)
        acc_b[0:rows, :] += dot_nn(act, w2_ref[...])
        d_exp = dexp[0:rows, :]
        d_act = dot_nt(d_exp, w2_ref[...]).astype(BF16).astype(F32)
        d_up = (d_act * gate_pre * sig).astype(BF16)
        d_gate = (d_act * up_pre * sig * (1.0 + gate_pre * (1.0 - sig))).astype(BF16)
        ring_1[slot] = dot_nn(xbt[:, 0:rows], d_gate)
        ring_3[slot] = dot_nn(xbt[:, 0:rows], d_up)
        ring_2[slot] = dot_tn(act, d_exp)
        dacc[0:rows, :] += dot_nt(d_gate, w1_ref[...]) + dot_nt(d_up, w3_ref[...])

    by_rows(1, run_b)
    for copy in leaving(step, slot):
        copy.start()
    by_rows(0, run_a)

    @pl.when(step + RING < pl.num_programs(0) * n_tile)
    def _():
        for copy in coming(step + RING, slot):
            copy.start()

    def return_a(rows):
        ra_ref[...] += wcol[:, 0:1] * dot_nn(put_a[:, 0:rows], acc_a[0:rows, :].astype(BF16))

    def return_b(rows):
        put = put_b[:, 0:rows]
        rb_ref[...] += dot_nn(put, dacc[0:rows, :].astype(BF16))
        out_b = dot_nn(put, acc_b[0:rows, :].astype(BF16))
        pick = jnp.sum(out_b * g_ref[...].astype(F32), axis=-1, keepdims=True)
        lane = lax.broadcasted_iota(jnp.int32, (n_tok, LANES), 1)
        dots[...] += jnp.where(lane == here, pick, 0.0)

    @pl.when(tile == pl.num_programs(1) - 1)
    def _():
        by_rows(0, return_a)
        by_rows(1, return_b)

    @pl.when(step == pl.num_programs(0) * n_tile - 1)
    def _():
        flat = dots[...].T
        n_src, n_exp, seq_len = rd_ref.shape
        for src in range(n_src):
            rd_ref[src] = flat[0:n_exp, src * seq_len:(src + 1) * seq_len]
        for back in range(RING - 1, -1, -1):
            for copy in leaving(step - back, lax.rem(step - back, RING)):
                copy.wait()


def tail_kernel(n_ep, n_pp, heads, ra_ref, rb_ref, rd_ref, ha_ref, hb_ref, n2b_ref, gb_ref, rtb_ref, x_ref, q_ref, k_ref, v_ref,
                p_ref, gain1_ref, gain2_ref, wq_ref, wk_ref, wv_ref, wo_ref, wr_ref,
                y_ref, dx_ref, dq_ref, dk_ref, dv_ref, dh_all, dg1_ref, sums_ref,
                near_b, swap_b, sum_b, far_b, near_a, swap_a, sum_a, far_a, near_d, swap_d, sum_d, far_d, small, small_1, small_2, small_3,
                y_own, dx_own, wq_s, wr_s, send_sem, recv_sem):
    me, partner, across, diag = ep_peers()
    stage = lax.axis_index('pp')
    later, earlier = lax.rem(stage + 1, n_pp), lax.rem(stage + n_pp - 1, n_pp)
    seq_len, d_model = y_ref.shape
    sems = (send_sem, recv_sem)
    near, over = {'ep': partner}, {'ep': across}
    greet((near, over, {'pp': later}, {'pp': earlier}))
    span = seq_len // CHUNKS
    parts = [pl.ds(c * span, span) for c in range(CHUNKS)]

    def chunked(src, dst, base, peer):
        return [push(src.at[part], dst.at[part], sems, base + c, peer) for c, part in enumerate(parts)]

    swap_b_c = chunked(rb_ref.at[diag], swap_b, 13, near)
    swap_a_c = chunked(ra_ref.at[diag], swap_a, 13 + CHUNKS, near)
    far_b_c = chunked(sum_b, far_b, 13 + 2 * CHUNKS, over)
    far_a_c = chunked(sum_a, far_a, 13 + 3 * CHUNKS, over)
    y_c = chunked(y_own, y_ref, 13 + 4 * CHUNKS, {'pp': later})
    swap_d_c = push(rd_ref.at[diag], swap_d, sems, 0, near)
    near_b_c = push(rb_ref.at[partner], near_b, sems, 1, near)
    near_d_c = push(rd_ref.at[partner], near_d, sems, 2, near)
    near_a_c = push(ra_ref.at[partner], near_a, sems, 3, near)
    far_d_c = push(sum_d, far_d, sems, 4, over)
    swap_d_c.start()
    for copy in swap_b_c:
        copy.start()
    for copy in (near_d_c, near_b_c, *swap_a_c, near_a_c):
        copy.start()
    swap_d_c.wait_recv()
    sum_d[...] = rd_ref[across] + swap_d[...]
    for c, part in enumerate(parts):
        swap_b_c[c].wait_recv()
        sum_b[part, :] = rb_ref[across, part, :] + swap_b[part, :]
        far_b_c[c].start()
        if c == 0:
            far_d_c.start()
    for c, part in enumerate(parts):
        swap_a_c[c].wait_recv()
        sum_a[part, :] = ra_ref[across, part, :] + swap_a[part, :]
        if c == 0:
            far_a_c[c].start()
    for h in range(heads):
        wq_s[:, h * LANES:(h + 1) * LANES] = wq_ref[h]
    wr_s[...] = jnp.zeros_like(wr_s)
    wr_s[0:wr_ref.shape[0], :] = wr_ref[...]

    gain1, gain2 = gain1_ref[...].astype(F32), gain2_ref[...].astype(F32)
    mine = pl.ds(pl.multiple_of(me * seq_len, seq_len), seq_len)
    route = rtb_ref[mine, :]
    id0, id1, gate0, gate1, keep0, keep1 = [route[:, i:i + 1] for i in range(6)]
    lane = lax.broadcasted_iota(jnp.int32, (seq_len, LANES), 1).astype(F32)
    hot0, hot1 = (lane == id0).astype(F32), (lane == id1).astype(F32)
    h_f32 = hb_ref[mine, :].astype(F32)
    inv = rms_inv(h_f32)
    h_hat = h_f32 * inv
    near_d_c.wait_recv()
    far_d_c.wait_recv()
    tile = rd_ref[me] + near_d[...] + far_d[...]
    dots = jnp.concatenate([tile, jnp.zeros((LANES - tile.shape[0], seq_len), F32)], axis=0).T
    d_gate0 = jnp.where(keep0 > 0, jnp.sum(hot0 * dots, axis=-1, keepdims=True), 0.0)
    d_gate1 = jnp.where(keep1 > 0, jnp.sum(hot1 * dots, axis=-1, keepdims=True), 0.0)
    mean_gate = gate0 * d_gate0 + gate1 * d_gate1
    d_logits = (hot0 * (gate0 * (d_gate0 - mean_gate)) + hot1 * (gate1 * (d_gate1 - mean_gate))).astype(BF16)
    d_routed = dot_nn(d_logits, wr_s[...])
    near_b_c.wait_recv()
    for copy in far_b_c:
        copy.wait_recv()
    d_normed = (rb_ref[me] + near_b[...] + far_b[...]) + d_routed
    d_hat = d_normed * gain2
    d_in = inv * (d_hat - h_hat * jnp.mean(d_hat * h_hat, axis=-1, keepdims=True))
    dh_all[me] = (d_in + gb_ref[me].astype(F32)).astype(BF16)
    dh_far = push(dh_all.at[me], dh_all.at[me], sems, 6, over)
    dh_near = push(dh_all.at[me], dh_all.at[me], sems, 7, near)
    dh_relay = push(dh_all.at[across], dh_all.at[across], sems, 8, near)
    dh_far.start()
    dh_near.start()
    for copy in far_a_c[1:]:
        copy.start()
    small[0:8, :] = dot_tn(d_logits, n2b_ref[mine, :])[0:8, :]
    small[8:16, :] = jnp.broadcast_to(jnp.sum(d_normed * h_hat, axis=0, keepdims=True), (8, d_model))
    small_near = push(small, small_1, sems, 9, near)
    small_near.start()

    head_dim = wk_ref.shape[1]

    def attention_back(s):
        rows = pl.ds(pl.multiple_of(s * seq_len, seq_len), seq_len)
        d_hid = dh_all[s]
        d_out = stack_heads(dot_nt(d_hid, wo_ref[...]).astype(BF16), heads, head_dim)
        probs = p_ref[s]
        d_probs = dot_nt(d_out, v_ref[rows, :])
        d_v = dot_tn(probs.astype(BF16), d_out).astype(BF16)
        d_scores = (probs * (d_probs - jnp.sum(probs * d_probs, axis=-1, keepdims=True)) * head_dim ** -0.5).astype(BF16)
        d_q = unstack_heads(dot_nn(d_scores, k_ref[rows, :]).astype(BF16), heads, seq_len)
        d_k = dot_tn(d_scores, stack_heads(q_ref[rows, :], heads, head_dim)).astype(BF16)
        dq_ref[rows, :], dk_ref[rows, :], dv_ref[rows, :] = d_q, d_k, d_v
        d_norm1 = dot_nt(d_q, wq_s[...]) + dot_nt(d_k, wk_ref[...]) + dot_nt(d_v, wv_ref[...])
        x_f32 = x_ref[s].astype(F32)
        inv1 = rms_inv(x_f32)
        x_hat = x_f32 * inv1
        dg1_ref[s] = jnp.broadcast_to(jnp.sum(d_norm1 * x_hat, axis=0, keepdims=True), (8, d_model))
        return d_hid, d_norm1, inv1, x_hat

    d_hid, d_norm1, inv1, x_hat = attention_back(me)
    d_hat1 = d_norm1 * gain1
    d_x = inv1 * (d_hat1 - x_hat * jnp.mean(d_hat1 * x_hat, axis=-1, keepdims=True)) + d_hid.astype(F32)
    dx_own[...] = d_x.astype(BF16)
    dx_c = push(dx_own, dx_ref, sems, 11, {'pp': earlier})
    dx_c.start()
    small_near.wait_recv()
    small_2[...] = small[...] + small_1[...]
    small_far = push(small_2, small_3, sems, 10, over)
    small_far.start()
    near_a_c.wait_recv()

    def leave_y(c):
        part = parts[c]
        far_a_c[c].wait_recv()
        own = pl.ds(pl.multiple_of(me * seq_len + c * span, span), span)
        y_own[part, :] = (ha_ref[own, :].astype(F32)
                          + (ra_ref[me, part, :] + near_a[part, :] + far_a[part, :])).astype(BF16)
        y_c[c].start()

    leave_y(0)
    dh_near.wait_recv()
    attention_back(partner)
    dh_far.wait_recv()
    dh_relay.start()
    leave_y(1)
    attention_back(across)
    leave_y(2)
    dh_relay.wait_recv()
    attention_back(diag)
    leave_y(3)
    small_far.wait_recv()
    sums_ref[...] = small_2[...] + small_3[...]
    dx_c.wait_recv()
    for copy in y_c:
        copy.wait_recv()
    for copy in (*swap_b_c, *swap_a_c, *far_b_c, *far_a_c, *y_c, swap_d_c, near_b_c, near_d_c, near_a_c, far_d_c, dh_far, dh_near,
                 dh_relay, small_near, small_far, dx_c):
        copy.wait_send()


def dense_kernel(n1_ref, o_ref, dq_ref, dk_ref, dv_ref, dh_ref, dg1_in, sums_in, y_in, dx_in,
                 dwq_ref, dwk_ref, dwv_ref, dwo_ref, dg1_ref, dg2_ref, dwr_ref, y_ref, dx_ref, n1t):
    step = pl.program_id(0)

    @pl.when(step == 0)
    def _():
        n1t[...] = n1_ref[...].astype(F32).T.astype(BF16)
        dwk_ref[...] = dot_nn(n1t[...], dk_ref[...])
        dwv_ref[...] = dot_nn(n1t[...], dv_ref[...])
        dg1_ref[...] = sum(dg1_in[s] for s in range(dg1_in.shape[0]))[0:1]
        dwr_ref[...] = sums_in[0:8, :]
        dg2_ref[...] = sums_in[8:9, :]
        y_ref[...] = y_in[...]
        dx_ref[...] = dx_in[...]

    pair = dot_nn(n1t[...], dq_ref[...])
    for i in range(dwq_ref.shape[0]):
        dwq_ref[i] = pair[:, i * LANES:(i + 1) * LANES]
    dwo_ref[...] = dot_tn(o_ref[...], dh_ref[...])


def shape_of(shape, dtype):
    return jax.ShapeDtypeStruct(shape, dtype)


def solution(mesh):
    n_ep, n_pp = mesh.shape['ep'], mesh.shape['pp']
    whole = pl.BlockSpec(memory_space=VMEM)

    def device_tick(x_a, x_b, g_b, ids_a, ids_b, count_a, count_b, gain_1, gain_2, w_q, w_k, w_v, w_o, w_r, w_1, w_3, w_2):
        seq_len, d_model = x_a.shape[2], x_a.shape[3]
        heads, head_dim = w_q.shape[2], w_q.shape[3]
        n_exp, e_local, ffn = w_r.shape[2], w_1.shape[1], w_1.shape[3]
        n_tok = n_ep * seq_len
        width = heads * head_dim
        xa, xb, gb = x_a[0, 0], x_b[0, 0], g_b[0, 0]
        wq = jnp.transpose(w_q[0], (1, 0, 2))
        wk, wv, wo = w_k[0, :, 0], w_v[0, :, 0], w_o[0].reshape(width, d_model)
        wr = jnp.transpose(w_r[0])
        tok, rows = (n_ep, seq_len, d_model), (n_tok, d_model)
        head_out = [shape_of(tok, BF16), shape_of(tok, BF16), shape_of(rows, BF16), shape_of(rows, BF16),
                    shape_of((n_tok, LANES), F32), shape_of((n_tok, LANES), F32), shape_of((n_tok, LANES), F32),
                    shape_of((n_tok, LANES), F32), shape_of((n_tok, LANES), F32), shape_of(rows, BF16), shape_of(rows, BF16),
                    shape_of(rows, BF16), shape_of((n_tok, width), BF16), shape_of((n_tok, head_dim), BF16),
                    shape_of((n_tok, head_dim), BF16), shape_of((n_ep, heads * seq_len, seq_len), F32),
                    shape_of((n_tok, width), BF16)]
        (xb_all, gb_all, n2a, n2b, wta, m_a, wtb, m_b, rtb, ha, hb, n1, q, k, v, probs, attn) = pl.pallas_call(
            functools.partial(head_kernel, n_ep, heads),
            out_shape=head_out,
            in_specs=[pl.BlockSpec(memory_space=pltpu.HBM)] * 14,
            out_specs=[whole] * len(head_out),
            scratch_shapes=[VMEM(tok, BF16), VMEM((8, LANES), jnp.int32), VMEM((n_ep, 8, LANES), jnp.int32),
                            VMEM((2, seq_len), jnp.int32), VMEM((2, seq_len), jnp.int32), VMEM((1, n_exp), jnp.int32),
                            VMEM((1, n_exp), jnp.int32), VMEM((1, d_model), BF16), VMEM((1, d_model), BF16),
                            VMEM((d_model, width), BF16), VMEM((d_model, head_dim), BF16), VMEM((d_model, head_dim), BF16),
                            VMEM((width, d_model), BF16), VMEM((n_exp, d_model), BF16), VMEM((LANES, d_model), BF16),
                            pltpu.SemaphoreType.DMA((13 + heads,)), pltpu.SemaphoreType.DMA((12,)),
                            pltpu.SemaphoreType.DMA((12,))],
            compiler_params=pltpu.CompilerParams(collective_id=0, has_side_effects=True, vmem_limit_bytes=HEAD_VMEM),
            name='head',
        )(*[pltpu.with_memory_space_constraint(arg, pltpu.HBM) for arg in (
            ids_a[0, 0].T, ids_b[0, 0].T, count_a[0], count_b[0], xa, xb, gb, gain_1, gain_2, wq, wk, wv, wo, wr)])

        n_tile = ffn // FFN_TILE

        def const(*shape):
            return pl.BlockSpec(shape, lambda e, f: (0,) * len(shape))
        hbm = pl.BlockSpec(memory_space=pltpu.HBM)
        r_a, r_b, r_d, dw1, dw3, dw2 = pl.pallas_call(
            functools.partial(moe_kernel, e_local),
            grid=(e_local, n_tile),
            out_shape=[shape_of(rows, F32), shape_of(rows, F32), shape_of((n_ep, n_exp, seq_len), F32), shape_of((e_local, d_model, ffn), F32),
                       shape_of((e_local, d_model, ffn), F32), shape_of((e_local, ffn, d_model), F32)],
            in_specs=[const(*rows)] * 3 + [const(n_tok, LANES)] * 4 + [hbm] * 3,
            out_specs=[const(*rows), const(*rows), const(n_ep, n_exp, seq_len), hbm, hbm, hbm],
            scratch_shapes=[VMEM(rows, BF16), VMEM(rows, BF16), VMEM((d_model, n_tok), BF16), VMEM(rows, BF16),
                            VMEM(rows, F32), VMEM(rows, F32), VMEM(rows, F32), VMEM((n_tok, n_tok), BF16),
                            VMEM((n_tok, n_tok), BF16), VMEM((n_tok, LANES), F32), VMEM((n_tok, LANES), F32), VMEM((RING, d_model, FFN_TILE), F32),
                            VMEM((RING, d_model, FFN_TILE), F32), VMEM((RING, FFN_TILE, d_model), F32),
                            VMEM((RING, d_model, FFN_TILE), BF16), VMEM((RING, d_model, FFN_TILE), BF16),
                            VMEM((RING, FFN_TILE, d_model), BF16), pltpu.SemaphoreType.DMA((RING, 3)),
                            pltpu.SemaphoreType.DMA((RING, 3)), pltpu.SMEM((2,), jnp.int32)],
            compiler_params=pltpu.CompilerParams(dimension_semantics=('arbitrary', 'arbitrary'),
                                                 vmem_limit_bytes=MOE_VMEM),
            name='moe',
        )(n2a, n2b, gb_all.reshape(rows), wta, m_a, wtb, m_b, w_1[0], w_3[0], w_2[0])

        small = (16, d_model)
        block = (seq_len, d_model)
        y_in, dx_in, dq, dk, dv, dh, dg1_in, sums = pl.pallas_call(
            functools.partial(tail_kernel, n_ep, n_pp, heads),
            out_shape=[shape_of(block, BF16), shape_of(block, BF16), shape_of((n_tok, width), BF16),
                       shape_of((n_tok, head_dim), BF16), shape_of((n_tok, head_dim), BF16), shape_of(tok, BF16),
                       shape_of((n_ep, 8, d_model), F32), shape_of(small, F32)],
            in_specs=[whole] * 20,
            out_specs=[whole] * 8,
            scratch_shapes=[VMEM(block, F32)] * 8 + [VMEM((n_exp, seq_len), F32)] * 4 + [VMEM(small, F32)] * 4
            + [VMEM(block, BF16), VMEM(block, BF16), VMEM((d_model, width), BF16), VMEM((LANES, d_model), BF16),
               pltpu.SemaphoreType.DMA((13 + 5 * CHUNKS,)), pltpu.SemaphoreType.DMA((13 + 5 * CHUNKS,))],
            compiler_params=pltpu.CompilerParams(collective_id=1, has_side_effects=True, vmem_limit_bytes=TAIL_VMEM),
            name='tail',
        )(r_a.reshape(tok), r_b.reshape(tok), r_d, ha, hb, n2b, gb_all, rtb, xb_all, q, k, v, probs,
          gain_1, gain_2, wq, wk, wv, wo, wr)

        pair = 2
        steps = heads // pair

        def held(*shape):
            return pl.BlockSpec(shape, lambda i: (0,) * len(shape))
        cols = pl.BlockSpec((n_tok, pair * head_dim), lambda i: (0, i))
        dwq, dwk, dwv, dwo, dg1, dg2, dwr, y_next, dx_prev = pl.pallas_call(
            dense_kernel,
            grid=(steps,),
            out_shape=[shape_of((heads, d_model, head_dim), F32), shape_of((d_model, head_dim), F32),
                       shape_of((d_model, head_dim), F32), shape_of((width, d_model), F32), shape_of((1, d_model), F32),
                       shape_of((1, d_model), F32), shape_of((n_exp, d_model), F32), shape_of(block, BF16), shape_of(block, BF16)],
            in_specs=[held(*rows), cols, cols, held(n_tok, head_dim), held(n_tok, head_dim), held(*rows),
                      held(n_ep, 8, d_model), held(*small), held(*block), held(*block)],
            out_specs=[pl.BlockSpec((pair, d_model, head_dim), lambda i: (i, 0, 0)), held(d_model, head_dim),
                       held(d_model, head_dim), pl.BlockSpec((pair * head_dim, d_model), lambda i: (i, 0)),
                       held(1, d_model), held(1, d_model), held(n_exp, d_model), held(*block), held(*block)],
            scratch_shapes=[VMEM((d_model, n_tok), BF16)],
            compiler_params=pltpu.CompilerParams(dimension_semantics=('arbitrary',), vmem_limit_bytes=DENSE_VMEM),
            name='dense',
        )(n1, attn, dq, dk, dv, dh.reshape(rows), dg1_in, sums, y_in, dx_in)
        return (y_next[None, None], dx_prev[None, None], dg1, dg2, jnp.transpose(dwq, (1, 0, 2))[None], dwk[None, :, None],
                dwv[None, :, None], dwo.reshape(w_o.shape), jnp.transpose(dwr)[None], dw1[None], dw3[None], dw2[None])

    tok_spec = P(('dp', 'pp'), 'ep', None, None)
    cnt_spec = P(('dp', 'pp'), 'ep', None)
    gain_spec = P('pp', None)
    attn_spec = P('pp', None, None, None)
    router_spec = P('pp', None, None)
    expert_spec = P('pp', 'ep', None, None)
    gain_out = P(('dp', 'pp'), None)
    attn_out_spec = P(('dp', 'pp'), None, None, None)
    router_out = P(('dp', 'pp'), None, None)
    expert_out_spec = P(('dp', 'pp'), 'ep', None, None)
    in_specs = (tok_spec, tok_spec, tok_spec, tok_spec, tok_spec, cnt_spec, cnt_spec, gain_spec, gain_spec,
                attn_spec, attn_spec, attn_spec, attn_spec, router_spec, expert_spec, expert_spec, expert_spec)
    out_specs = (tok_spec, tok_spec, gain_out, gain_out, attn_out_spec, attn_out_spec, attn_out_spec, attn_out_spec,
                 router_out, expert_out_spec, expert_out_spec, expert_out_spec)
    return jax.shard_map(device_tick, mesh=mesh, in_specs=in_specs, out_specs=out_specs, check_vma=False)
```

profile of v0, /device:TPU:2, one launch (start us, length us, event | category | flops | bytes accessed | tf_op | source)
XLA Modules:
  0.0 102.3 jit_solution(15774066231051605119)
XLA Ops:
  0.6 18.8 %head.1 = (bf16[4,128,768]{2,1,0:T(8,128)(2,1)S(1)}, bf16[4,128,768]{2,1,0:T(8,128)(2,1)S(1)}, bf16[512,768]{1,0:T(8,128)(2,1)S(1)}, bf16[512,768]{1,0:T(8,128)(...) custom-call(s32[2,128]{1,0:T(2,128)} %bitcast.65, ...), custom_call_target="tpu_custom_call" | custom-call | tf_op jit(solution)/shard_map/head/pallas_call | solution.py:580
  19.5 0.0 copy-start
  19.5 0.0 copy-start.1
  19.5 0.0 copy-start.2
  19.5 0.0 copy-start.3
  19.5 0.0 copy-start.4
  19.5 0.0 copy-start.5
  19.6 0.0 copy-start.6
  19.6 38.5 %moe.1 = (f32[512,768]{1,0:T(8,128)S(1)}, f32[512,768]{1,0:T(8,128)S(1)}, f32[4,8,128]{2,1,0:T(8,128)S(1)}, f32[2,768,2048]{2,1,0:T(8,128)}, f32[2,768,2048]{2,1,0:T(8,128)}, /*index=5*/f32[2,2048,768]{2,1,0:T(8,128)}) custom-call(bf16[512,768]{1,0:T(8,128)(2,1)S(1)} %get-tuple-element.54.n2a_ref, bf16[512,768]{1,0:T(8,128)(2,1)S(1)} %get-tuple-element.55.n2b_ref, ...), custom_call_target="tpu_custom_call" | custom-call | tf_op jit(solution)/shard_map/moe/pallas_call | solution.py:602
  58.1 0.0 copy-done
  58.1 0.0 copy-done.1
  58.1 0.0 copy-done.2
  58.1 0.0 copy-done.3
  58.1 0.0 copy-done.4
  58.1 0.0 copy-done.5
  58.1 0.0 copy-done.6
  58.1 40.0 %tail.1 = (bf16[128,768]{1,0:T(8,128)(2,1)S(1)}, bf16[128,768]{1,0:T(8,128)(2,1)S(1)}, bf16[512,768]{1,0:T(8,128)(2,1)S(1)}, bf16[512,128]{1,0:T(8,128)(2,1)S(1)...) custom-call(f32[4,128,768]{2,1,0:T(8,128)S(1)} %bitcast.50, ...), custom_call_target="tpu_custom_call" | custom-call | tf_op jit(solution)/shard_map/tail/pallas_call | solution.py:623
  98.1 4.2 %dense.1 = (f32[6,768,128]{2,1,0:T(8,128)}, f32[768,128]{1,0:T(8,128)}, f32[768,128]{1,0:T(8,128)}, f32[768,768]{1,0:T(8,128)}, f32[1,768]{1,0:T(1,128)}, /*inde...) custom-call(bf16[512,768]{1,0:T(8,128)(2,1)S(1)} %get-tuple-element.52.n1_ref, ...), custom_call_target="tpu_custom_call" | custom-call | tf_op jit(solution)/shard_map/dense/pallas_call | solution.py:644
Async XLA Ops:
  19.5 38.6 %copy-start = (bf16[1,768,6,128]{3,1,2,0:T(8,128)(2,1)S(1)}, bf16[1,768,6,128]{3,1,2,0:T(8,128)(2,1)}, u32[]{:S(2)}) copy-start(bf16[1,768,6,128]{3,1,2,0:T(8,128)(2,1)} %param.26) | copy-start | bytes 3538948
  19.5 38.6 %copy-start.1 = (bf16[1,6,128,768]{3,2,1,0:T(8,128)(2,1)S(1)}, bf16[1,6,128,768]{3,2,1,0:T(8,128)(2,1)}, u32[]{:S(2)}) copy-start(bf16[1,6,128,768]{3,2,1,0:T(8,128)(2,1)} %param.29) | copy-start | bytes 3538948
  19.5 38.6 %copy-start.2 = (bf16[1,768,1,128]{3,1,2,0:T(8,128)(2,1)S(1)}, bf16[1,768,1,128]{3,1,2,0:T(8,128)(2,1)}, u32[]{:S(2)}) copy-start(bf16[1,768,1,128]{3,1,2,0:T(8,128)(2,1)} %param.27) | copy-start | bytes 589828
  19.5 38.6 %copy-start.3 = (bf16[1,768,1,128]{3,1,2,0:T(8,128)(2,1)S(1)}, bf16[1,768,1,128]{3,1,2,0:T(8,128)(2,1)}, u32[]{:S(2)}) copy-start(bf16[1,768,1,128]{3,1,2,0:T(8,128)(2,1)} %param.28) | copy-start | bytes 589828
  19.5 38.6 %copy-start.4 = (bf16[1,768,8]{1,2,0:T(8,128)(2,1)S(1)}, bf16[1,768,8]{1,2,0:T(8,128)(2,1)}, u32[]{:S(2)}) copy-start(bf16[1,768,8]{1,2,0:T(8,128)(2,1)} %param.30) | copy-start | bytes 36868
  19.5 38.6 %copy-start.5 = (bf16[1,768]{1,0:T(2,128)(2,1)S(1)}, bf16[1,768]{1,0:T(2,128)(2,1)}, u32[]{:S(2)}) copy-start(bf16[1,768]{1,0:T(2,128)(2,1)} %gain1_ref.1) | copy-start | bytes 4612
  19.6 38.6 %copy-start.6 = (bf16[1,768]{1,0:T(2,128)(2,1)S(1)}, bf16[1,768]{1,0:T(2,128)(2,1)}, u32[]{:S(2)}) copy-start(bf16[1,768]{1,0:T(2,128)(2,1)} %gain2_ref.1) | copy-start | bytes 4612
where the time goes:
time: 101 us; the launch traced here: 102 us
  Pallas kernels  101 us (100%)
    pallas_call x1, Pallas kernels, device_tick(): pl.pallas_call(functools.partial(tail_kernel, n_ep, n_pp, heads), out_sha...  40 us
    pallas_call x1, Pallas kernels, device_tick(): pl.pallas_call(functools.partial(moe_kernel, e_local), grid=(e_local, n_t...  38.5 us
    pallas_call x1, Pallas kernels, device_tick(): pl.pallas_call(functools.partial(head_kernel, n_ep, heads), out_shape=hea...  18.8 us
    pallas_call x1, Pallas kernels, device_tick(): pl.pallas_call(dense_kernel, grid=(steps,), out_shape=[shape_of((heads, d...  4.17 us

commit v1 on v0

--- a/solution.py
+++ b/solution.py
@@ -13,10 +13,11 @@
 BF16 = jnp.bfloat16
 MESH = pl.DeviceIdType.MESH
 VMEM = pltpu.VMEM
-FFN_TILE = 256
+FFN_TILE = 512
 LANES = 128
 ROW_SIZES = (128, 192, 320, 512)
-RING = 3
+MOVE_SIZES = (192, 512)
+RING = 2
 CHUNKS = 4
 HEAD_VMEM = 34 * 2 ** 20
 MOE_VMEM = 44 * 2 ** 20
@@ -232,8 +233,8 @@
 
 
 def moe_kernel(e_local, n2a_ref, n2b_ref, g_ref, wta_ref, ma_ref, wtb_ref, mb_ref, w1_hbm, w3_hbm, w2_hbm,
-               ra_ref, rb_ref, rd_ref, dw1_ref, dw3_ref, dw2_ref, x_a, x_b, xbt, dexp, acc_a, acc_b, dacc, put_a, put_b, wcol, dots, ring_1, ring_3, ring_2,
-               w1_all, w3_all, w2_all, ring_sem, load_sem, blocks):
+               ra_ref, rb_ref, rd_ref, dw1_ref, dw3_ref, dw2_ref, x_a, x_b, xbt, dexp, acc_a, acc_b, dacc, put_a, put_b, wcol, dots, ring_13, ring_2,
+               w13_all, w2_all, ring_sem, load_sem, blocks):
     expert, tile = pl.program_id(0), pl.program_id(1)
     n_tile = pl.num_programs(1)
     step = expert * n_tile + tile
@@ -242,15 +243,15 @@
     def leaving(step, slot):
         expert, start = step // n_tile, pl.multiple_of(lax.rem(step, n_tile) * FFN_TILE, FFN_TILE)
         span = pl.ds(start, FFN_TILE)
-        return [pltpu.make_async_copy(ring_1.at[slot], dw1_ref.at[expert, :, span], ring_sem.at[slot, 0]),
-                pltpu.make_async_copy(ring_3.at[slot], dw3_ref.at[expert, :, span], ring_sem.at[slot, 1]),
+        return [pltpu.make_async_copy(ring_13.at[slot, :, 0:FFN_TILE], dw1_ref.at[expert, :, span], ring_sem.at[slot, 0]),
+                pltpu.make_async_copy(ring_13.at[slot, :, FFN_TILE:2 * FFN_TILE], dw3_ref.at[expert, :, span], ring_sem.at[slot, 1]),
                 pltpu.make_async_copy(ring_2.at[slot], dw2_ref.at[expert, span, :], ring_sem.at[slot, 2])]
 
     def coming(step, slot):
         expert, start = step // n_tile, pl.multiple_of(lax.rem(step, n_tile) * FFN_TILE, FFN_TILE)
         span = pl.ds(start, FFN_TILE)
-        return [pltpu.make_async_copy(w1_hbm.at[expert, :, span], w1_all.at[slot], load_sem.at[slot, 0]),
-                pltpu.make_async_copy(w3_hbm.at[expert, :, span], w3_all.at[slot], load_sem.at[slot, 1]),
+        return [pltpu.make_async_copy(w1_hbm.at[expert, :, span], w13_all.at[slot, :, 0:FFN_TILE], load_sem.at[slot, 0]),
+                pltpu.make_async_copy(w3_hbm.at[expert, :, span], w13_all.at[slot, :, FFN_TILE:2 * FFN_TILE], load_sem.at[slot, 1]),
                 pltpu.make_async_copy(w2_hbm.at[expert, span, :], w2_all.at[slot], load_sem.at[slot, 2])]
 
     @pl.when(step == 0)
@@ -262,9 +263,11 @@
     n_tok, d_model = n2a_ref.shape
     here = lax.axis_index('ep') * e_local + expert
 
-    def by_rows(which, work):
-        for rows in ROW_SIZES:
-            pl.when(blocks[which] == rows)(functools.partial(work, rows))
+    def by_rows(which, work, sizes=ROW_SIZES):
+        below = 0
+        for rows in sizes:
+            pl.when((blocks[which] > below) & (blocks[which] <= rows))(functools.partial(work, rows))
+            below = rows
 
     @pl.when(tile == 0)
     def _():
@@ -305,8 +308,8 @@
             acc_b[0:rows, :] = jnp.zeros((rows, d_model), F32)
             dacc[0:rows, :] = jnp.zeros((rows, d_model), F32)
 
-        by_rows(0, fetch_a)
-        by_rows(1, fetch_b)
+        by_rows(0, fetch_a, MOVE_SIZES)
+        by_rows(1, fetch_b, MOVE_SIZES)
 
     @pl.when((tile == 0) & (expert == 0))
     def _():
@@ -322,10 +325,11 @@
         for copy in leaving(step - RING, slot):
             copy.wait()
 
-    w1_ref, w3_ref, w2_ref = w1_all.at[slot], w3_all.at[slot], w2_all.at[slot]
+    w13_ref, w2_ref = w13_all.at[slot], w2_all.at[slot]
 
     def forward(x, rows):
-        gate_pre, up_pre = dot_nn(x[0:rows, :], w1_ref[...]), dot_nn(x[0:rows, :], w3_ref[...])
+        both = dot_nn(x[0:rows, :], w13_ref[...])
+        gate_pre, up_pre = both[:, 0:FFN_TILE], both[:, FFN_TILE:]
         sig = jax.nn.sigmoid(gate_pre)
         return gate_pre, up_pre, sig, (gate_pre * sig * up_pre).astype(BF16)
 
@@ -340,10 +344,10 @@
         d_act = dot_nt(d_exp, w2_ref[...]).astype(BF16).astype(F32)
         d_up = (d_act * gate_pre * sig).astype(BF16)
         d_gate = (d_act * up_pre * sig * (1.0 + gate_pre * (1.0 - sig))).astype(BF16)
-        ring_1[slot] = dot_nn(xbt[:, 0:rows], d_gate)
-        ring_3[slot] = dot_nn(xbt[:, 0:rows], d_up)
+        d_both = jnp.concatenate([d_gate, d_up], axis=1)
+        ring_13[slot] = dot_nn(xbt[:, 0:rows], d_both)
         ring_2[slot] = dot_tn(act, d_exp)
-        dacc[0:rows, :] += dot_nt(d_gate, w1_ref[...]) + dot_nt(d_up, w3_ref[...])
+        dacc[0:rows, :] += dot_nt(d_both, w13_ref[...])
 
     by_rows(1, run_b)
     for copy in leaving(step, slot):
@@ -368,8 +372,8 @@
 
     @pl.when(tile == pl.num_programs(1) - 1)
     def _():
-        by_rows(0, return_a)
-        by_rows(1, return_b)
+        by_rows(0, return_a, MOVE_SIZES)
+        by_rows(1, return_b, MOVE_SIZES)
 
     @pl.when(step == pl.num_programs(0) * n_tile - 1)
     def _():
@@ -608,9 +612,8 @@
             out_specs=[const(*rows), const(*rows), const(n_ep, n_exp, seq_len), hbm, hbm, hbm],
             scratch_shapes=[VMEM(rows, BF16), VMEM(rows, BF16), VMEM((d_model, n_tok), BF16), VMEM(rows, BF16),
                             VMEM(rows, F32), VMEM(rows, F32), VMEM(rows, F32), VMEM((n_tok, n_tok), BF16),
-                            VMEM((n_tok, n_tok), BF16), VMEM((n_tok, LANES), F32), VMEM((n_tok, LANES), F32), VMEM((RING, d_model, FFN_TILE), F32),
-                            VMEM((RING, d_model, FFN_TILE), F32), VMEM((RING, FFN_TILE, d_model), F32),
-                            VMEM((RING, d_model, FFN_TILE), BF16), VMEM((RING, d_model, FFN_TILE), BF16),
+                            VMEM((n_tok, n_tok), BF16), VMEM((n_tok, LANES), F32), VMEM((n_tok, LANES), F32), VMEM((RING, d_model, 2 * FFN_TILE), F32),
+                            VMEM((RING, FFN_TILE, d_model), F32), VMEM((RING, d_model, 2 * FFN_TILE), BF16),
                             VMEM((RING, FFN_TILE, d_model), BF16), pltpu.SemaphoreType.DMA((RING, 3)),
                             pltpu.SemaphoreType.DMA((RING, 3)), pltpu.SMEM((2,), jnp.int32)],
             compiler_params=pltpu.CompilerParams(dimension_semantics=('arbitrary', 'arbitrary'),

time: 101 us -> 90.9 us (0.900)
  the two profiles are of different devices: /device:TPU:2 before, /device:TPU:0 now
where the time goes in v1:
time: 90.9 us; the launch traced here: 90.4 us
  Pallas kernels  89.6 us (99%)
    pallas_call x1, Pallas kernels, device_tick(): pl.pallas_call(functools.partial(tail_kernel, n_ep, n_pp, heads), out_sha...  35.3 us
    pallas_call x1, Pallas kernels, device_tick(): pl.pallas_call(functools.partial(moe_kernel, e_local), grid=(e_local, n_t...  29.8 us
    pallas_call x1, Pallas kernels, device_tick(): pl.pallas_call(functools.partial(head_kernel, n_ep, heads), out_shape=hea...  20.3 us
    pallas_call x1, Pallas kernels, device_tick(): pl.pallas_call(dense_kernel, grid=(steps,), out_shape=[shape_of((heads, d...  4.17 us

profile of v1, /device:TPU:0, one launch (start us, length us, event | category | flops | bytes accessed | tf_op | source)
XLA Modules:
  0.0 90.4 jit_solution(7951941804608266647)
XLA Ops:
  0.6 20.3 %head.1 = (bf16[4,128,768]{2,1,0:T(8,128)(2,1)S(1)}, bf16[4,128,768]{2,1,0:T(8,128)(2,1)S(1)}, bf16[512,768]{1,0:T(8,128)(2,1)S(1)}, bf16[512,768]{1,0:T(8,128)(...) custom-call(s32[2,128]{1,0:T(2,128)} %bitcast.65, ...), custom_call_target="tpu_custom_call" | custom-call | tf_op jit(solution)/shard_map/head/pallas_call | solution.py:584
  21.0 0.0 copy-start
  21.0 0.0 copy-start.1
  21.0 0.0 copy-start.2
  21.0 0.0 copy-start.3
  21.0 0.0 copy-start.4
  21.1 0.0 copy-start.5
  21.1 0.0 copy-start.6
  21.1 29.8 %moe.1 = (f32[512,768]{1,0:T(8,128)S(1)}, f32[512,768]{1,0:T(8,128)S(1)}, f32[4,8,128]{2,1,0:T(8,128)S(1)}, f32[2,768,2048]{2,1,0:T(8,128)}, f32[2,768,2048]{2,1,0:T(8,128)}, /*index=5*/f32[2,2048,768]{2,1,0:T(8,128)}) custom-call(bf16[512,768]{1,0:T(8,128)(2,1)S(1)} %get-tuple-element.54.n2a_ref, bf16[512,768]{1,0:T(8,128)(2,1)S(1)} %get-tuple-element.55.n2b_ref, ...), custom_call_target="tpu_custom_call" | custom-call | tf_op jit(solution)/shard_map/moe/pallas_call | solution.py:606
  50.9 0.0 copy-done
  50.9 0.0 copy-done.1
  50.9 0.0 copy-done.2
  50.9 0.0 copy-done.3
  50.9 0.0 copy-done.4
  50.9 0.0 copy-done.5
  50.9 0.0 copy-done.6
  50.9 35.3 %tail.1 = (bf16[128,768]{1,0:T(8,128)(2,1)S(1)}, bf16[128,768]{1,0:T(8,128)(2,1)S(1)}, bf16[512,768]{1,0:T(8,128)(2,1)S(1)}, bf16[512,128]{1,0:T(8,128)(2,1)S(1)...) custom-call(f32[4,128,768]{2,1,0:T(8,128)S(1)} %bitcast.50, ...), custom_call_target="tpu_custom_call" | custom-call | tf_op jit(solution)/shard_map/tail/pallas_call | solution.py:626
  86.2 4.2 %dense.1 = (f32[6,768,128]{2,1,0:T(8,128)}, f32[768,128]{1,0:T(8,128)}, f32[768,128]{1,0:T(8,128)}, f32[768,768]{1,0:T(8,128)}, f32[1,768]{1,0:T(1,128)}, /*inde...) custom-call(bf16[512,768]{1,0:T(8,128)(2,1)S(1)} %get-tuple-element.52.n1_ref, ...), custom_call_target="tpu_custom_call" | custom-call | tf_op jit(solution)/shard_map/dense/pallas_call | solution.py:647
Async XLA Ops:
  21.0 29.9 %copy-start = (bf16[1,768,6,128]{3,1,2,0:T(8,128)(2,1)S(1)}, bf16[1,768,6,128]{3,1,2,0:T(8,128)(2,1)}, u32[]{:S(2)}) copy-start(bf16[1,768,6,128]{3,1,2,0:T(8,128)(2,1)} %param.26) | copy-start | bytes 3538948
  21.0 29.9 %copy-start.1 = (bf16[1,6,128,768]{3,2,1,0:T(8,128)(2,1)S(1)}, bf16[1,6,128,768]{3,2,1,0:T(8,128)(2,1)}, u32[]{:S(2)}) copy-start(bf16[1,6,128,768]{3,2,1,0:T(8,128)(2,1)} %param.29) | copy-start | bytes 3538948
  21.0 29.9 %copy-start.2 = (bf16[1,768,1,128]{3,1,2,0:T(8,128)(2,1)S(1)}, bf16[1,768,1,128]{3,1,2,0:T(8,128)(2,1)}, u32[]{:S(2)}) copy-start(bf16[1,768,1,128]{3,1,2,0:T(8,128)(2,1)} %param.27) | copy-start | bytes 589828
  21.0 29.9 %copy-start.3 = (bf16[1,768,1,128]{3,1,2,0:T(8,128)(2,1)S(1)}, bf16[1,768,1,128]{3,1,2,0:T(8,128)(2,1)}, u32[]{:S(2)}) copy-start(bf16[1,768,1,128]{3,1,2,0:T(8,128)(2,1)} %param.28) | copy-start | bytes 589828
  21.0 29.9 %copy-start.4 = (bf16[1,768,8]{1,2,0:T(8,128)(2,1)S(1)}, bf16[1,768,8]{1,2,0:T(8,128)(2,1)}, u32[]{:S(2)}) copy-start(bf16[1,768,8]{1,2,0:T(8,128)(2,1)} %param.30) | copy-start | bytes 36868
  21.1 29.9 %copy-start.5 = (bf16[1,768]{1,0:T(2,128)(2,1)S(1)}, bf16[1,768]{1,0:T(2,128)(2,1)}, u32[]{:S(2)}) copy-start(bf16[1,768]{1,0:T(2,128)(2,1)} %gain1_ref.1) | copy-start | bytes 4612
  21.1 29.9 %copy-start.6 = (bf16[1,768]{1,0:T(2,128)(2,1)S(1)}, bf16[1,768]{1,0:T(2,128)(2,1)}, u32[]{:S(2)}) copy-start(bf16[1,768]{1,0:T(2,128)(2,1)} %gain2_ref.1) | copy-start | bytes 4612
